TPU v7x, 128 devices: a whole 4x4x4 slice. The times are simulated.
128 devices in a mesh: node: 8 (over y_hi, z), slab: 16 (over y_lo, x, core).
Axes of the slice: x: 4, y: 4 (y_hi: 2, y_lo: 2; y = y_hi * 2 + y_lo), z: 4, core: 2. Of those that a mesh axis runs over, the one named last changes fastest.
Arguments:
- initial: float32 [64, 256, 256], P('slab'), may hold values from -20 to 20
- sections: float32 [8, 64, 256, 256], P('node', 'slab'), may hold values from -21 to 21
Outputs:
- new_sections: float32 [8, 64, 256, 256], P('node', 'slab')
- residual_max: float32 [3], replicated
All inputs are finite; a program needn't handle non-finite values.
Results may differ from a plain program's by a relative error of at most 0.0003.
Values sent between devices are 32-bit elements; how exact they have to be, the bound alone decides.
A program may use at most 64 MiB of HBM per device.

v0:
```python
import functools
import math

import jax
import jax.numpy as jnp
import numpy as np
from jax import lax
from jax.experimental import pallas as pl
from jax.experimental.pallas import tpu as pltpu
from jax.sharding import Mesh
from jax.sharding import PartitionSpec as P

SWEEPS = 3
AXES = ("node_0", "node_1", "slab_0", "slab_1", "slab_2")
SLAB = ("slab_0", "slab_1", "slab_2")
NODE = ("node_0", "node_1")
MESH = pl.DeviceIdType.MESH
F32 = jnp.float32
BF16 = jnp.bfloat16
STEP = 4.0
NODES = 8
SLABS = 16
DEVS = NODES * SLABS
CELLS = 256
FIELDS = SWEEPS + 1


def radau_value(order, point):
    prev_value = 1.0
    prev_slope = 0.0
    this_value = point
    this_slope = 1.0
    for degree in range(1, order):
        next_value = ((2 * degree + 1) * point * this_value - degree * prev_value) / (degree + 1)
        next_slope = (
            (2 * degree + 1) * (this_value + point * this_slope) - degree * prev_slope
        ) / (degree + 1)
        prev_value, prev_slope = (this_value, this_slope)
        this_value, this_slope = (next_value, next_slope)
    return (this_value - prev_value, this_slope - prev_slope)


def radau_tables(node_total):
    points = []
    for node_index in range(node_total):
        estimate = math.cos(2.0 * math.pi * node_index / (2 * node_total - 1))
        if node_index > 0:
            for repeat in range(60):
                poly_value, poly_slope = radau_value(node_total, estimate)
                estimate = estimate - poly_value / poly_slope
        points.append((estimate + 1.0) / 2.0)
    points = sorted(points)
    quadrature = []
    for row_index in range(node_total):
        entries = []
        for column_index in range(node_total):
            coeffs = [1.0]
            for other_index in range(node_total):
                if other_index != column_index:
                    divisor = points[column_index] - points[other_index]
                    shifted = [0.0] + coeffs
                    widened = coeffs + [0.0]
                    coeffs = [
                        (shifted[place] - points[other_index] * widened[place]) / divisor
                        for place in range(len(shifted))
                    ]
            integral = 0.0
            for place in range(len(coeffs)):
                integral = integral + coeffs[place] * points[row_index] ** (place + 1) / (place + 1)
            entries.append(integral)
        quadrature.append(entries)
    return (points, quadrature)


def cas_table(length):
    indices = np.arange(length)
    phases = (indices[:, None] * indices[None, :] % length) * (2.0 * math.pi / length)
    return (np.cos(phases) + np.sin(phases)) / math.sqrt(length)


def eigen_line(length):
    return -4.0 * np.sin(np.arange(length) * (math.pi / length)) ** 2


def halves(table):
    high = table.astype(np.float32).astype(BF16)
    low = (table - high.astype(np.float64)).astype(np.float32).astype(BF16)
    return high, low


def tables():
    line = cas_table(CELLS)
    high, low = halves(line)
    right = np.concatenate([high, high, low], 0)
    left = np.concatenate([high, high, low], 1)
    cas_x = cas_table(64)
    cross = np.zeros((2, 64, SLABS, 2, 4))
    for row in range(2):
        cross[row, :, :, row, :] = cas_x.reshape(64, SLABS, 4)
    cross = cross.reshape(128, 128)
    high, low = halves(cross)
    forward = np.concatenate([high, high, low], 1)
    high, low = halves(cross.T)
    back = np.concatenate([high, high, low], 1)
    lam_x = np.broadcast_to((STEP * eigen_line(64))[:, None], (64, 128)).astype(np.float32)
    lam_z = np.broadcast_to((STEP * eigen_line(CELLS)).reshape(2, 1, 128), (2, 8, 128)).astype(np.float32)
    lam_y = (STEP * eigen_line(CELLS)).astype(np.float32)
    return right, left, forward, back, lam_x, lam_z, lam_y


def split(value, axis):
    high = value.astype(BF16)
    low = (value - high.astype(F32)).astype(BF16)
    return jnp.concatenate([high, low, high], axis)


def matmul(a, b):
    return jnp.dot(a, b, preferred_element_type=F32)


def kernel(
    points, quadrature,
    sec_hbm, ini_hbm, right_hbm, left_hbm, fwd_hbm, back_hbm, lam_x_hbm, lam_z_hbm, lam_y_ref,
    out_hbm, res_ref,
    sec, ini, right, left, fwd, back, lam_x, lam_z,
    rows, rows0, sent, sent0, got, got0, modes, modes0, spect, bsent, bgot, out, peak_sent, peak_got,
    in_sem, send_sem, send0_sem, got_sem, got0_sem, bsend_sem, bgot_sem, psend_sem, pgot_sem, out_sem,
):
    here = tuple(lax.axis_index(a) for a in AXES)
    my_node = here[0] * 4 + here[1]
    my_slab = (here[2] * 4 + here[3]) * 2 + here[4]
    me = my_node * SLABS + my_slab
    my_y = here[0] * 2 + here[2]

    loads = [
        pltpu.make_async_copy(src, dst, in_sem.at[i])
        for i, (src, dst) in enumerate([
            (left_hbm, left), (sec_hbm.at[0], sec), (right_hbm, right), (ini_hbm, ini), (fwd_hbm, fwd),
            (back_hbm, back), (lam_x_hbm, lam_x), (lam_z_hbm, lam_z),
        ])
    ]
    for load in loads:
        load.start()

    def target(k):
        y = lax.rem(my_y + k // 32, 4)
        return (
            y // 2,
            lax.rem(here[1] + lax.rem(k // 8, 4), 4),
            lax.rem(y, 2),
            lax.rem(here[3] + lax.rem(k // 2, 4), 4),
            lax.rem(here[4] + lax.rem(k, 2), 2),
        )

    def flat(t):
        return (((t[0] * 4 + t[1]) * 2 + t[2]) * 4 + t[3]) * 2 + t[4]

    barrier = pltpu.get_barrier_semaphore()

    def greet(k, carry):
        pl.semaphore_signal(barrier, inc=1, device_id=target(k), device_id_type=MESH)
        return carry

    lax.fori_loop(1, DEVS, greet, 0)

    def put(buf, x, count, value):
        for h in range(2):
            buf[h, pl.ds(x, count, stride=4), :] = value[:, 128 * h : 128 * h + 128]

    loads[0].wait()
    loads[1].wait()
    for x in range(4):
        put(rows, x, CELLS, matmul(left[...], split(sec[x], 0)))
    loads[2].wait()
    for b in range(4):
        part = jnp.concatenate([rows[h, pl.ds(CELLS * b, CELLS), :] for h in range(2)], 1)
        part = matmul(split(part, 1), right[...])
        for h in range(2):
            sent[h, pl.ds(32 * b, 32)] = part[:, 128 * h : 128 * h + 128].reshape(32, 8, 128)
    loads[3].wait()
    mine = left[pl.ds(pl.multiple_of(my_node * 32, 32), 32), :]
    for x in range(4):
        put(rows0, x, 32, matmul(mine, split(ini[x], 0)))
    part = jnp.concatenate([rows0[h] for h in range(2)], 1)
    part = matmul(split(part, 1), right[...])
    for h in range(2):
        sent0[h] = part[:, 128 * h : 128 * h + 128].reshape(16, 8, 128)

    pl.semaphore_wait(barrier, DEVS - 1)

    def spread(src, dst, s_sem, r_sem):
        def one(j, carry):
            t = target(lax.rem(j * 37, DEVS))
            pltpu.make_async_remote_copy(
                src.at[flat(t)], dst.at[me], s_sem, r_sem, device_id=t, device_id_type=MESH
            ).start()
            return carry

        lax.fori_loop(1, DEVS, one, 0)
        dst[me] = src[me]

    def all_but_one(buf, count, sem):
        view = buf.at[pl.ds(0, count - 1)]
        pltpu.make_async_copy(view, view, sem).wait()

    for h in range(2):
        def one(k, carry):
            yl = lax.rem(here[2] + k // 8, 2)
            x = lax.rem(here[3] + lax.rem(k // 2, 4), 4)
            c = lax.rem(here[4] + lax.rem(k, 2), 2)
            pltpu.make_async_remote_copy(
                sent0.at[h, (yl * 4 + x) * 2 + c], got0.at[h, my_slab], send0_sem.at[h], got0_sem.at[h],
                device_id=(here[0], here[1], yl, x, c), device_id_type=MESH,
            ).start()
            return carry

        lax.fori_loop(1, SLABS, one, 0)
        got0[h, my_slab] = sent0[h, my_slab]
        spread(sent.at[h], got.at[h], send_sem.at[h], got_sem.at[h])

    for load in loads[4:]:
        load.wait()

    def sweeps(h):
        all_but_one(got0.at[h], SLABS, got0_sem.at[h])
        all_but_one(got.at[h], DEVS, got_sem.at[h])
        modes0[...] = matmul(fwd[...], split(got0[h].reshape(128, 128), 0))
        for n in range(NODES):
            block = got[h, pl.ds(SLABS * n, SLABS)].reshape(128, 128)
            modes[:, 128 * n : 128 * n + 128] = matmul(fwd[...], split(block, 0))
        for row in range(2):
            lam_y = lam_y_ref[2 * me + row]

            def one(i, carry):
                r = pl.multiple_of(64 * row + 8 * i, 8)
                lam = lam_x[pl.ds(pl.multiple_of(8 * i, 8), 8), :] + lam_z[h] + lam_y
                start = modes0[pl.ds(r, 8), :]
                value = [modes[pl.ds(r, 8), 128 * m : 128 * m + 128] for m in range(NODES)]
                for k in range(SWEEPS):
                    slope = [lam * v for v in value]
                    after = []
                    for m in range(NODES):
                        total = start - value[m]
                        for j in range(NODES):
                            total = total + quadrature[m][j] * slope[j]
                        spect[k, pl.ds(r, 8), 128 * m : 128 * m + 128] = total
                        after.append(value[m] + total / (1.0 - (points[m] / (k + 1.0)) * lam))
                    value = after
                for m in range(NODES):
                    spect[SWEEPS, pl.ds(r, 8), 128 * m : 128 * m + 128] = value[m]
                return carry

            lax.fori_loop(0, 8, one, 0)

    def give(f, h):
        for n in range(NODES):
            block = matmul(back[...], split(spect[f, :, 128 * n : 128 * n + 128], 0))
            bsent[f, h, pl.ds(SLABS * n, SLABS)] = block.reshape(SLABS, 8, 128)
        spread(bsent.at[f, h], bgot.at[f, h], bsend_sem.at[f, h], bgot_sem.at[f, h])

    for h in range(2):
        sweeps(h)
        for f in range(FIELDS):
            give(f, h)

    def take(f):
        for h in range(2):
            all_but_one(bgot.at[f, h], DEVS, bgot_sem.at[f, h])
        for b in range(4):
            part = jnp.concatenate(
                [bgot[f, h, pl.ds(32 * b, 32)].reshape(CELLS, 128) for h in range(2)], 1
            )
            part = matmul(split(part, 1), right[...])
            for h in range(2):
                rows[h, pl.ds(CELLS * b, CELLS), :] = part[:, 128 * h : 128 * h + 128]
        for x in range(4):
            part = jnp.concatenate([rows[h, pl.ds(x, CELLS, stride=4), :] for h in range(2)], 1)
            yield x, matmul(left[...], split(part, 0))

    lane = lax.broadcasted_iota(jnp.int32, (1, 128), 1)
    peaks = jnp.zeros((1, 128), F32)
    for f in range(SWEEPS):
        top = None
        for x, field in take(f):
            field = jnp.max(jnp.abs(field).reshape(32, 8, CELLS), axis=0)
            top = field if top is None else jnp.maximum(top, field)
        peaks = jnp.where(lane == f, jnp.max(top), peaks)
    peak_sent[...] = peaks

    def tell(j, carry):
        pltpu.make_async_remote_copy(
            peak_sent, peak_got.at[me], psend_sem, pgot_sem,
            device_id=target(lax.rem(j * 37, DEVS)), device_id_type=MESH,
        ).start()
        return carry

    lax.fori_loop(1, DEVS, tell, 0)
    peak_got[me] = peaks
    for x, field in take(SWEEPS):
        out[x] = field
        pltpu.make_async_copy(out.at[x], out_hbm.at[0, x], out_sem.at[x]).start()

    all_but_one(peak_got, DEVS, pgot_sem)
    peaks = jnp.max(peak_got[...], axis=0)
    for f in range(SWEEPS):
        res_ref[f] = jnp.max(jnp.where(lane == f, peaks, 0.0))

    for h in range(2):
        all_but_one(sent0.at[h], SLABS, send0_sem.at[h])
        all_but_one(sent.at[h], DEVS, send_sem.at[h])
        for f in range(FIELDS):
            all_but_one(bsent.at[f, h], DEVS, bsend_sem.at[f, h])
    all_but_one(peak_got, DEVS, psend_sem)
    for x in range(4):
        pltpu.make_async_copy(out.at[x], out_hbm.at[0, x], out_sem.at[x]).wait()


def on_device(initial, sections):
    points, quadrature = radau_tables(NODES)
    any_space = pl.BlockSpec(memory_space=pl.ANY)
    smem = pl.BlockSpec(memory_space=pltpu.SMEM)
    dma = pltpu.SemaphoreType.DMA
    parts = [jnp.asarray(t) for t in tables()]
    vmem = pltpu.VMEM
    new, peak = pl.pallas_call(
        functools.partial(kernel, points, quadrature),
        out_shape=(
            jax.ShapeDtypeStruct(sections.shape, F32),
            jax.ShapeDtypeStruct((SWEEPS,), F32),
        ),
        in_specs=[any_space] * 8 + [smem],
        out_specs=(any_space, smem),
        scratch_shapes=[
            vmem((4, CELLS, CELLS), F32),
            vmem((4, CELLS, CELLS), F32),
            vmem((3 * CELLS, CELLS), BF16),
            vmem((CELLS, 3 * CELLS), BF16),
            vmem((128, 384), BF16),
            vmem((128, 384), BF16),
            vmem((64, 128), F32),
            vmem((2, 8, 128), F32),
            vmem((2, 4 * CELLS, 128), F32),
            vmem((2, 128, 128), F32),
            vmem((2, DEVS, 8, 128), F32),
            vmem((2, SLABS, 8, 128), F32),
            vmem((2, DEVS, 8, 128), F32),
            vmem((2, SLABS, 8, 128), F32),
            vmem((128, NODES * 128), F32),
            vmem((128, 128), F32),
            vmem((FIELDS, 128, NODES * 128), F32),
            vmem((FIELDS, 2, DEVS, 8, 128), F32),
            vmem((FIELDS, 2, DEVS, 8, 128), F32),
            vmem((4, CELLS, CELLS), F32),
            vmem((1, 128), F32),
            vmem((DEVS, 1, 128), F32),
            dma((8,)),
            dma((2,)),
            dma((2,)),
            dma((2,)),
            dma((2,)),
            dma((FIELDS, 2)),
            dma((FIELDS, 2)),
            dma,
            dma,
            dma((4,)),
        ],
        compiler_params=pltpu.CompilerParams(
            collective_id=0, has_side_effects=True, vmem_limit_bytes=48 << 20
        ),
        name="sdc",
    )(sections, initial, *parts)
    return new, peak


def solution(mesh):
    torus = Mesh(mesh.devices.reshape(2, 4, 2, 4, 2), AXES)
    return jax.shard_map(
        on_device,
        mesh=torus,
        in_specs=(P(SLAB, None, None), P(NODE, SLAB, None, None)),
        out_specs=(P(NODE, SLAB, None, None), P()),
        check_vma=False,
    )
```

profile of v0, /device:TPU:1, one launch (start us, length us, event | category | flops | bytes accessed | tf_op | source)
XLA Modules:
  0.0 100.8 jit_solution(17387374129493667993)
XLA Ops:
  0.6 0.0 copy-start.7
  0.6 0.0 copy-start.8
  0.7 0.7 copy-done.7
  1.3 0.0 copy-done.8
  1.3 0.0 copy-start
  1.3 1.2 %copy-done = f32[1,4,256,256]{3,2,1,0:T(8,128)S(1)} copy-done((f32[1,4,256,256]{3,2,1,0:T(8,128)S(1)}, f32[1,4,256,256]{3,2,1,0:T(8,128)}, u32[]{:S(2)}) %copy-start) | copy-done | bytes 1048600
  2.6 0.0 copy-start.1
  2.6 1.2 %copy-done.1 = f32[4,256,256]{2,1,0:T(8,128)S(1)} copy-done((f32[4,256,256]{2,1,0:T(8,128)S(1)}, f32[4,256,256]{2,1,0:T(8,128)}, u32[]{:S(2)}) %copy-start.1) | copy-done | bytes 1048600
  3.8 0.0 copy-start.2
  3.8 1.0 copy-done.2
  4.8 0.0 copy-start.3
  4.8 1.0 copy-done.3
  5.8 0.0 copy-start.4
  5.8 0.9 copy-done.4
  6.7 0.0 copy-start.5
  6.7 0.9 copy-done.5
  7.6 0.0 copy-start.6
  7.6 0.8 copy-done.6
  8.3 91.0 %sdc.1 = (f32[1,4,256,256]{3,2,1,0:T(8,128)S(1)}, f32[3]{0:T(128)S(1)}) custom-call(f32[1,4,256,256]{3,2,1,0:T(8,128)S(1)} %copy-done, f32[4,256,256]{2,1,0:T(8,128)S(1)} %copy-done.1, bf16[768,256]{1,0:T(8,128)(2,1)S(1)} %copy-done.3, bf16[256,768]{1,0:T(8,128)(2,1)S(1)} %copy-done.2, bf16[128,384]{1,0:T(8,128)(2,1)S(1)} %copy-done.5, ...), custom_call_target="tpu_custom_call" | custom-call | tf_op jit(solution)/shard_map/sdc/pallas_call | solution.py:325
  99.4 1.0 copy.13
  100.3 0.5 copy.14
Async XLA Ops:
  0.6 0.7 copy-start.7
  0.6 0.7 copy-start.8
  1.3 1.2 %copy-start = (f32[1,4,256,256]{3,2,1,0:T(8,128)S(1)}, f32[1,4,256,256]{3,2,1,0:T(8,128)}, u32[]{:S(2)}) copy-start(f32[1,4,256,256]{3,2,1,0:T(8,128)} %sec_hbm.1) | copy-start | bytes 3145732
  2.6 1.2 %copy-start.1 = (f32[4,256,256]{2,1,0:T(8,128)S(1)}, f32[4,256,256]{2,1,0:T(8,128)}, u32[]{:S(2)}) copy-start(f32[4,256,256]{2,1,0:T(8,128)} %ini_hbm.1) | copy-start | bytes 3145732
  3.8 1.0 copy-start.2
  4.8 1.0 copy-start.3
  5.8 0.9 copy-start.4
  6.7 0.9 copy-start.5
  7.6 0.8 copy-start.6
where the time goes:
time: 101 us
  Pallas kernels  91 us (90%)
  local copies, waits for them, and re-layouts  9.15 us (9%)
    pallas_call x1, Pallas kernels, on_device(): pl.pallas_call(functools.partial(kernel, points, quadrature), out_shape=(...  91 us
    unnamed x20, local copies, waits for them, and re-layouts  9.15 us

commit v1 on v0

--- a/solution.py
+++ b/solution.py
@@ -104,7 +104,7 @@
     back = np.concatenate([high, high, low], 1)
     lam_x = np.broadcast_to((STEP * eigen_line(64))[:, None], (64, 128)).astype(np.float32)
     lam_z = np.broadcast_to((STEP * eigen_line(CELLS)).reshape(2, 1, 128), (2, 8, 128)).astype(np.float32)
-    lam_y = (STEP * eigen_line(CELLS)).astype(np.float32)
+    lam_y = np.broadcast_to((STEP * eigen_line(CELLS)).reshape(DEVS, 2, 1), (DEVS, 2, 128)).astype(np.float32)
     return right, left, forward, back, lam_x, lam_z, lam_y
 
 
@@ -120,9 +120,9 @@
 
 def kernel(
     points, quadrature,
-    sec_hbm, ini_hbm, right_hbm, left_hbm, fwd_hbm, back_hbm, lam_x_hbm, lam_z_hbm, lam_y_ref,
+    sec_hbm, ini_hbm, right_hbm, left_hbm, fwd_hbm, back_hbm, lam_x_hbm, lam_z_hbm, lam_y_hbm,
     out_hbm, res_ref,
-    sec, ini, right, left, fwd, back, lam_x, lam_z,
+    sec, ini, right, left, fwd, back, lam_x, lam_z, lam_y,
     rows, rows0, sent, sent0, got, got0, modes, modes0, spect, bsent, bgot, out, peak_sent, peak_got,
     in_sem, send_sem, send0_sem, got_sem, got0_sem, bsend_sem, bgot_sem, psend_sem, pgot_sem, out_sem,
 ):
@@ -136,32 +136,38 @@
         pltpu.make_async_copy(src, dst, in_sem.at[i])
         for i, (src, dst) in enumerate([
             (left_hbm, left), (sec_hbm.at[0], sec), (right_hbm, right), (ini_hbm, ini), (fwd_hbm, fwd),
-            (back_hbm, back), (lam_x_hbm, lam_x), (lam_z_hbm, lam_z),
+            (back_hbm, back), (lam_x_hbm, lam_x), (lam_z_hbm, lam_z), (lam_y_hbm.at[me], lam_y),
         ])
     ]
     for load in loads:
         load.start()
 
-    def target(k):
-        y = lax.rem(my_y + k // 32, 4)
-        return (
-            y // 2,
-            lax.rem(here[1] + lax.rem(k // 8, 4), 4),
-            lax.rem(y, 2),
-            lax.rem(here[3] + lax.rem(k // 2, 4), 4),
-            lax.rem(here[4] + lax.rem(k, 2), 2),
-        )
-
     def flat(t):
         return (((t[0] * 4 + t[1]) * 2 + t[2]) * 4 + t[3]) * 2 + t[4]
 
+    cores = (here[4], 1 - here[4])
+    planes = [lax.rem(my_y + k, 4) for k in range(4)]
+    planes = [(y // 2, lax.rem(y, 2)) for y in planes]
+    depths = [lax.rem(here[1] + k, 4) for k in range(4)]
+
+    def others(visit, low=0, high=4):
+        def step(i, first):
+            along = [lax.rem(here[3] + i + k, 4) for k in range(4)]
+            for k in range(first, 32):
+                y_high, y_low = planes[5 * k % 16 // 4]
+                visit((y_high, depths[5 * k % 4], y_low, along[k % 4], cores[k // 16]))
+
+        def body(i, carry):
+            step(i, 0)
+            return carry
+
+        if low == 0:
+            step(0, 1)
+        lax.fori_loop(max(low, 1), high, body, 0)
+
     barrier = pltpu.get_barrier_semaphore()
 
-    def greet(k, carry):
-        pl.semaphore_signal(barrier, inc=1, device_id=target(k), device_id_type=MESH)
-        return carry
-
-    lax.fori_loop(1, DEVS, greet, 0)
+    others(lambda t: pl.semaphore_signal(barrier, inc=1, device_id=t, device_id_type=MESH))
 
     def put(buf, x, count, value):
         for h in range(2):
@@ -177,6 +183,23 @@
         part = matmul(split(part, 1), right[...])
         for h in range(2):
             sent[h, pl.ds(32 * b, 32)] = part[:, 128 * h : 128 * h + 128].reshape(32, 8, 128)
+    pl.semaphore_wait(barrier, DEVS - 1)
+
+    def spread(src, dst, s_sem, r_sem, low=0, high=4):
+        others(
+            lambda t: pltpu.make_async_remote_copy(
+                src.at[flat(t)], dst.at[me], s_sem, r_sem, device_id=t, device_id_type=MESH
+            ).start(),
+            low, high,
+        )
+        if low == 0:
+            dst[me] = src[me]
+
+    def all_but_one(buf, count, sem):
+        view = buf.at[pl.ds(0, count - 1)]
+        pltpu.make_async_copy(view, view, sem).wait()
+
+    spread(sent.at[0], got.at[0], send_sem.at[0], got_sem.at[0])
     loads[3].wait()
     mine = left[pl.ds(pl.multiple_of(my_node * 32, 32), 32), :]
     for x in range(4):
@@ -186,37 +209,16 @@
     for h in range(2):
         sent0[h] = part[:, 128 * h : 128 * h + 128].reshape(16, 8, 128)
 
-    pl.semaphore_wait(barrier, DEVS - 1)
-
-    def spread(src, dst, s_sem, r_sem):
-        def one(j, carry):
-            t = target(lax.rem(j * 37, DEVS))
+    for h in range(2):
+        for k in range(1, SLABS):
+            x = lax.rem(here[3] + k, 4)
+            t = (here[0], here[1], here[2] if k < 8 else 1 - here[2], x, cores[k // 4 % 2])
             pltpu.make_async_remote_copy(
-                src.at[flat(t)], dst.at[me], s_sem, r_sem, device_id=t, device_id_type=MESH
+                sent0.at[h, (t[2] * 4 + t[3]) * 2 + t[4]], got0.at[h, my_slab], send0_sem.at[h], got0_sem.at[h],
+                device_id=t, device_id_type=MESH,
             ).start()
-            return carry
-
-        lax.fori_loop(1, DEVS, one, 0)
-        dst[me] = src[me]
-
-    def all_but_one(buf, count, sem):
-        view = buf.at[pl.ds(0, count - 1)]
-        pltpu.make_async_copy(view, view, sem).wait()
-
-    for h in range(2):
-        def one(k, carry):
-            yl = lax.rem(here[2] + k // 8, 2)
-            x = lax.rem(here[3] + lax.rem(k // 2, 4), 4)
-            c = lax.rem(here[4] + lax.rem(k, 2), 2)
-            pltpu.make_async_remote_copy(
-                sent0.at[h, (yl * 4 + x) * 2 + c], got0.at[h, my_slab], send0_sem.at[h], got0_sem.at[h],
-                device_id=(here[0], here[1], yl, x, c), device_id_type=MESH,
-            ).start()
-            return carry
-
-        lax.fori_loop(1, SLABS, one, 0)
         got0[h, my_slab] = sent0[h, my_slab]
-        spread(sent.at[h], got.at[h], send_sem.at[h], got_sem.at[h])
+    spread(sent.at[1], got.at[1], send_sem.at[1], got_sem.at[1])
 
     for load in loads[4:]:
         load.wait()
@@ -229,11 +231,11 @@
             block = got[h, pl.ds(SLABS * n, SLABS)].reshape(128, 128)
             modes[:, 128 * n : 128 * n + 128] = matmul(fwd[...], split(block, 0))
         for row in range(2):
-            lam_y = lam_y_ref[2 * me + row]
+            lam_0 = lam_z[h] + lam_y[row : row + 1, :]
 
             def one(i, carry):
                 r = pl.multiple_of(64 * row + 8 * i, 8)
-                lam = lam_x[pl.ds(pl.multiple_of(8 * i, 8), 8), :] + lam_z[h] + lam_y
+                lam = lam_x[pl.ds(pl.multiple_of(8 * i, 8), 8), :] + lam_0
                 start = modes0[pl.ds(r, 8), :]
                 value = [modes[pl.ds(r, 8), 128 * m : 128 * m + 128] for m in range(NODES)]
                 for k in range(SWEEPS):
@@ -252,16 +254,26 @@
 
             lax.fori_loop(0, 8, one, 0)
 
-    def give(f, h):
+    def make(f, h):
         for n in range(NODES):
             block = matmul(back[...], split(spect[f, :, 128 * n : 128 * n + 128], 0))
             bsent[f, h, pl.ds(SLABS * n, SLABS)] = block.reshape(SLABS, 8, 128)
-        spread(bsent.at[f, h], bgot.at[f, h], bsend_sem.at[f, h], bgot_sem.at[f, h])
-
-    for h in range(2):
-        sweeps(h)
-        for f in range(FIELDS):
-            give(f, h)
+
+    def give(f, h, low=0, high=4):
+        spread(bsent.at[f, h], bgot.at[f, h], bsend_sem.at[f, h], bgot_sem.at[f, h], low, high)
+
+    sweeps(0)
+    for f in range(2):
+        make(f, 0)
+        give(f, 0)
+    for f in range(2, FIELDS):
+        make(f, 0)
+    sweeps(1)
+    for f in range(FIELDS):
+        make(f, 1)
+        if f >= 2:
+            give(f, 0)
+        give(f, 1, 0, 4 if f < SWEEPS else 2)
 
     def take(f):
         for h in range(2):
@@ -287,15 +299,13 @@
         peaks = jnp.where(lane == f, jnp.max(top), peaks)
     peak_sent[...] = peaks
 
-    def tell(j, carry):
-        pltpu.make_async_remote_copy(
-            peak_sent, peak_got.at[me], psend_sem, pgot_sem,
-            device_id=target(lax.rem(j * 37, DEVS)), device_id_type=MESH,
+    others(
+        lambda t: pltpu.make_async_remote_copy(
+            peak_sent, peak_got.at[me], psend_sem, pgot_sem, device_id=t, device_id_type=MESH
         ).start()
-        return carry
-
-    lax.fori_loop(1, DEVS, tell, 0)
+    )
     peak_got[me] = peaks
+    give(SWEEPS, 1, 2, 4)
     for x, field in take(SWEEPS):
         out[x] = field
         pltpu.make_async_copy(out.at[x], out_hbm.at[0, x], out_sem.at[x]).start()
@@ -328,7 +338,7 @@
             jax.ShapeDtypeStruct(sections.shape, F32),
             jax.ShapeDtypeStruct((SWEEPS,), F32),
         ),
-        in_specs=[any_space] * 8 + [smem],
+        in_specs=[any_space] * 9,
         out_specs=(any_space, smem),
         scratch_shapes=[
             vmem((4, CELLS, CELLS), F32),
@@ -339,6 +349,7 @@
             vmem((128, 384), BF16),
             vmem((64, 128), F32),
             vmem((2, 8, 128), F32),
+            vmem((2, 128), F32),
             vmem((2, 4 * CELLS, 128), F32),
             vmem((2, 128, 128), F32),
             vmem((2, DEVS, 8, 128), F32),
@@ -353,7 +364,7 @@
             vmem((4, CELLS, CELLS), F32),
             vmem((1, 128), F32),
             vmem((DEVS, 1, 128), F32),
-            dma((8,)),
+            dma((9,)),
             dma((2,)),
             dma((2,)),
             dma((2,)),
@@ -365,7 +376,7 @@
             dma((4,)),
         ],
         compiler_params=pltpu.CompilerParams(
-            collective_id=0, has_side_effects=True, vmem_limit_bytes=48 << 20
+            collective_id=0, has_side_effects=True, vmem_limit_bytes=67043328
         ),
         name="sdc",
     )(sections, initial, *parts)

time: 101 us -> 79.8 us (0.79)
  Pallas kernels: 91 us -> 76.2 us
  local copies, waits for them, and re-layouts: 9.15 us -> 2.8 us
    pallas_call x1, Pallas kernels: 91 us -> 76.2 us  [on_device(): pl.pallas_call(functools.partial(kernel, points, quadrature), out_shape=(...]
    unnamed x20 -> x4, local copies, waits for them, and re-layouts: 9.15 us -> 2.8 us
where the time goes in v1:
time: 79.8 us; the launch traced here: 79.6 us
  Pallas kernels  76.2 us (95%)
  local copies, waits for them, and re-layouts  2.8 us (4%)
    pallas_call x1, Pallas kernels, on_device(): pl.pallas_call(functools.partial(kernel, points, quadrature), out_shape=(...  76.2 us
    unnamed x4, local copies, waits for them, and re-layouts  2.8 us

profile of v1, /device:TPU:1, one launch (start us, length us, event | category | flops | bytes accessed | tf_op | source)
XLA Modules:
  0.0 79.6 jit_solution(17848382787616078586)
XLA Ops:
  0.6 76.2 %sdc.1 = (f32[1,4,256,256]{3,2,1,0:T(8,128)}, f32[3]{0:T(128)}) custom-call(f32[1,4,256,256]{3,2,1,0:T(8,128)} %sec_hbm.1, f32[4,256,256]{2,1,0:T(8,128)} %ini_hbm.1, bf16[768,256]{1,0:T(8,128)(2,1)} %constant.14.clone.right_hbm, bf16[256,768]{1,0:T(8,128)(2,1)} %constant.15.clone.left_hbm, bf16[128,384]{1,0:T(8,128)(2,1)} %constant.16.clone.fwd_hbm, ...), custom_call_target="tpu_custom_call" | custom-call | tf_op jit(solution)/shard_map/sdc/pallas_call | solution.py:335
  76.8 0.0 copy-start
  76.8 2.3 %copy.13 = f32[1,4,256,256]{3,2,1,0:T(8,128)} copy(f32[1,4,256,256]{3,2,1,0:T(8,128)} %get-tuple-element.4) | data formatting | bytes 2097152
  79.1 0.0 copy-done
  79.1 0.5 copy.14
Async XLA Ops:
  76.8 2.3 %copy-start = (f32[3]{0:T(128)S(1)}, f32[3]{0:T(128)}, u32[]{:S(2)}) copy-start(f32[3]{0:T(128)} %get-tuple-element.5) | copy-start | bytes 40

commit v2 on v1

--- a/solution.py
+++ b/solution.py
@@ -23,6 +23,12 @@
 DEVS = NODES * SLABS
 CELLS = 256
 FIELDS = SWEEPS + 1
+HOPS = (0, 1, 2, 1)
+FAR_FIRST = sorted(
+    ((k // 4 % 4, k % 4, (k + k // 16) % 4, k // 64) for k in (37 * j % DEVS for j in range(DEVS))),
+    key=lambda offset: -sum(HOPS[step] for step in offset[:3]),
+)
+FAR_FIRST.remove((0, 0, 0, 0))
 
 
 def radau_value(order, point):
@@ -91,7 +97,7 @@
 def tables():
     line = cas_table(CELLS)
     high, low = halves(line)
-    right = np.concatenate([high, high, low], 0)
+    right = np.concatenate([part for h in (slice(0, 128), slice(128, 256)) for part in (high[h], high[h], low[h])], 0)
     left = np.concatenate([high, high, low], 1)
     cas_x = cas_table(64)
     cross = np.zeros((2, 64, SLABS, 2, 4))
@@ -114,6 +120,10 @@
     return jnp.concatenate([high, low, high], axis)
 
 
+def split_halves(first, second):
+    return jnp.concatenate([split(first, 1), split(second, 1)], 1)
+
+
 def matmul(a, b):
     return jnp.dot(a, b, preferred_element_type=F32)
 
@@ -121,10 +131,10 @@
 def kernel(
     points, quadrature,
     sec_hbm, ini_hbm, right_hbm, left_hbm, fwd_hbm, back_hbm, lam_x_hbm, lam_z_hbm, lam_y_hbm,
-    out_hbm, res_ref,
+    base, last, peak, right_b,
     sec, ini, right, left, fwd, back, lam_x, lam_z, lam_y,
-    rows, rows0, sent, sent0, got, got0, modes, modes0, spect, bsent, bgot, out, peak_sent, peak_got,
-    in_sem, send_sem, send0_sem, got_sem, got0_sem, bsend_sem, bgot_sem, psend_sem, pgot_sem, out_sem,
+    rows, rows0, sent, sent0, got, got0, modes, modes0, spect, bsent, bgot, peak_sent, peak_got,
+    in_sem, send_sem, send0_sem, got_sem, got0_sem, bsend_sem, bgot_sem, psend_sem, pgot_sem,
 ):
     here = tuple(lax.axis_index(a) for a in AXES)
     my_node = here[0] * 4 + here[1]
@@ -137,6 +147,7 @@
         for i, (src, dst) in enumerate([
             (left_hbm, left), (sec_hbm.at[0], sec), (right_hbm, right), (ini_hbm, ini), (fwd_hbm, fwd),
             (back_hbm, back), (lam_x_hbm, lam_x), (lam_z_hbm, lam_z), (lam_y_hbm.at[me], lam_y),
+            (right_hbm.at[pl.ds(384, 384)], right_b),
         ])
     ]
     for load in loads:
@@ -148,6 +159,7 @@
     cores = (here[4], 1 - here[4])
     planes = [lax.rem(my_y + k, 4) for k in range(4)]
     planes = [(y // 2, lax.rem(y, 2)) for y in planes]
+    across = [lax.rem(here[3] + k, 4) for k in range(4)]
     depths = [lax.rem(here[1] + k, 4) for k in range(4)]
 
     def others(visit, low=0, high=4):
@@ -165,9 +177,13 @@
             step(0, 1)
         lax.fori_loop(max(low, 1), high, body, 0)
 
+    def far_first(visit, low=0, high=DEVS - 1):
+        for y, z, x, core in FAR_FIRST[low:high]:
+            visit((planes[y][0], depths[z], planes[y][1], across[x], cores[core]))
+
     barrier = pltpu.get_barrier_semaphore()
 
-    others(lambda t: pl.semaphore_signal(barrier, inc=1, device_id=t, device_id_type=MESH))
+    far_first(lambda t: pl.semaphore_signal(barrier, inc=1, device_id=t, device_id_type=MESH))
 
     def put(buf, x, count, value):
         for h in range(2):
@@ -179,20 +195,20 @@
         put(rows, x, CELLS, matmul(left[...], split(sec[x], 0)))
     loads[2].wait()
     for b in range(4):
-        part = jnp.concatenate([rows[h, pl.ds(CELLS * b, CELLS), :] for h in range(2)], 1)
-        part = matmul(split(part, 1), right[...])
+        part = split_halves(*(rows[h, pl.ds(CELLS * b, CELLS), :] for h in range(2)))
+        part = matmul(part, right[...])
         for h in range(2):
             sent[h, pl.ds(32 * b, 32)] = part[:, 128 * h : 128 * h + 128].reshape(32, 8, 128)
     pl.semaphore_wait(barrier, DEVS - 1)
 
-    def spread(src, dst, s_sem, r_sem, low=0, high=4):
-        others(
+    def spread(src, dst, s_sem, r_sem, order=others, low=None, high=None):
+        order(
             lambda t: pltpu.make_async_remote_copy(
                 src.at[flat(t)], dst.at[me], s_sem, r_sem, device_id=t, device_id_type=MESH
             ).start(),
-            low, high,
+            *(() if low is None else (low, high)),
         )
-        if low == 0:
+        if not low:
             dst[me] = src[me]
 
     def all_but_one(buf, count, sem):
@@ -204,8 +220,7 @@
     mine = left[pl.ds(pl.multiple_of(my_node * 32, 32), 32), :]
     for x in range(4):
         put(rows0, x, 32, matmul(mine, split(ini[x], 0)))
-    part = jnp.concatenate([rows0[h] for h in range(2)], 1)
-    part = matmul(split(part, 1), right[...])
+    part = matmul(split_halves(rows0[0], rows0[1]), right[...])
     for h in range(2):
         sent0[h] = part[:, 128 * h : 128 * h + 128].reshape(16, 8, 128)
 
@@ -220,126 +235,152 @@
         got0[h, my_slab] = sent0[h, my_slab]
     spread(sent.at[1], got.at[1], send_sem.at[1], got_sem.at[1])
 
-    for load in loads[4:]:
+    for load in loads[4:9]:
         load.wait()
 
-    def sweeps(h):
+    def enter(h):
         all_but_one(got0.at[h], SLABS, got0_sem.at[h])
         all_but_one(got.at[h], DEVS, got_sem.at[h])
         modes0[...] = matmul(fwd[...], split(got0[h].reshape(128, 128), 0))
-        for n in range(NODES):
-            block = got[h, pl.ds(SLABS * n, SLABS)].reshape(128, 128)
-            modes[:, 128 * n : 128 * n + 128] = matmul(fwd[...], split(block, 0))
-        for row in range(2):
-            lam_0 = lam_z[h] + lam_y[row : row + 1, :]
-
-            def one(i, carry):
+        for n in range(0, NODES, 2):
+            pair = [got[h, pl.ds(SLABS * (n + k), SLABS)].reshape(128, 128) for k in range(2)]
+            modes[:, 128 * n : 128 * n + 256] = matmul(fwd[...], split(jnp.concatenate(pair, 1), 0))
+
+    def sweep(k, h):
+        lam_0 = [lam_z[h] + lam_y[row : row + 1, :] for row in range(2)]
+
+        def one(i, carry):
+            lam_1 = lam_x[pl.ds(pl.multiple_of(8 * i, 8), 8), :]
+            for row in range(2):
                 r = pl.multiple_of(64 * row + 8 * i, 8)
-                lam = lam_x[pl.ds(pl.multiple_of(8 * i, 8), 8), :] + lam_0
+                lam = lam_1 + lam_0[row]
                 start = modes0[pl.ds(r, 8), :]
                 value = [modes[pl.ds(r, 8), 128 * m : 128 * m + 128] for m in range(NODES)]
-                for k in range(SWEEPS):
-                    slope = [lam * v for v in value]
-                    after = []
-                    for m in range(NODES):
-                        total = start - value[m]
-                        for j in range(NODES):
-                            total = total + quadrature[m][j] * slope[j]
-                        spect[k, pl.ds(r, 8), 128 * m : 128 * m + 128] = total
-                        after.append(value[m] + total / (1.0 - (points[m] / (k + 1.0)) * lam))
-                    value = after
+                slope = [lam * v for v in value]
                 for m in range(NODES):
-                    spect[SWEEPS, pl.ds(r, 8), 128 * m : 128 * m + 128] = value[m]
-                return carry
-
-            lax.fori_loop(0, 8, one, 0)
+                    total = start - value[m]
+                    for j in range(NODES):
+                        total = total + quadrature[m][j] * slope[j]
+                    spect[pl.ds(r, 8), 128 * m : 128 * m + 128] = total
+                    modes[pl.ds(r, 8), 128 * m : 128 * m + 128] = value[m] + total / (
+                        1.0 - (points[m] / (k + 1.0)) * lam
+                    )
+            return carry
+
+        lax.fori_loop(0, 8, one, 0)
 
     def make(f, h):
-        for n in range(NODES):
-            block = matmul(back[...], split(spect[f, :, 128 * n : 128 * n + 128], 0))
-            bsent[f, h, pl.ds(SLABS * n, SLABS)] = block.reshape(SLABS, 8, 128)
-
-    def give(f, h, low=0, high=4):
-        spread(bsent.at[f, h], bgot.at[f, h], bsend_sem.at[f, h], bgot_sem.at[f, h], low, high)
-
-    sweeps(0)
-    for f in range(2):
+        source = spect if f < SWEEPS else modes
+        for n in range(0, NODES, 2):
+            pair = matmul(back[...], split(source[:, 128 * n : 128 * n + 256], 0))
+            for k in range(2):
+                block = pair[:, 128 * k : 128 * k + 128].reshape(SLABS, 8, 128)
+                bsent[f, h, pl.ds(SLABS * (n + k), SLABS)] = block
+
+    def give(f, h, *how):
+        spread(bsent.at[f, h], bgot.at[f, h], bsend_sem.at[f, h], bgot_sem.at[f, h], *how)
+
+    enter(0)
+    for f in range(FIELDS):
+        if f < SWEEPS:
+            sweep(f, 0)
         make(f, 0)
-        give(f, 0)
-    for f in range(2, FIELDS):
-        make(f, 0)
-    sweeps(1)
+        if f < 2:
+            give(f, 0)
+    enter(1)
     for f in range(FIELDS):
+        if f < SWEEPS:
+            sweep(f, 1)
         make(f, 1)
         if f >= 2:
             give(f, 0)
-        give(f, 1, 0, 4 if f < SWEEPS else 2)
-
-    def take(f):
-        for h in range(2):
-            all_but_one(bgot.at[f, h], DEVS, bgot_sem.at[f, h])
-        for b in range(4):
-            part = jnp.concatenate(
-                [bgot[f, h, pl.ds(32 * b, 32)].reshape(CELLS, 128) for h in range(2)], 1
-            )
-            part = matmul(split(part, 1), right[...])
-            for h in range(2):
-                rows[h, pl.ds(CELLS * b, CELLS), :] = part[:, 128 * h : 128 * h + 128]
-        for x in range(4):
-            part = jnp.concatenate([rows[h, pl.ds(x, CELLS, stride=4), :] for h in range(2)], 1)
-            yield x, matmul(left[...], split(part, 0))
+        give(f, 1, *(() if f < SWEEPS else (far_first, 0, 48)))
+
+    def ready(f, h):
+        all_but_one(bgot.at[f, h], DEVS, bgot_sem.at[f, h])
+
+    def plane(f, h, x):
+        return bgot.at[f, h].reshape(4 * CELLS, 128)[pl.ds(x, CELLS, stride=4), :]
+
+    def pairs(h):
+        for x in range(0, 4, 2):
+            part = jnp.concatenate([plane(SWEEPS, h, x + k) for k in range(2)], 1)
+            part = matmul(left[...], split(part, 0))
+            yield x, part[:, :128]
+            yield x + 1, part[:, 128:]
 
     lane = lax.broadcasted_iota(jnp.int32, (1, 128), 1)
     peaks = jnp.zeros((1, 128), F32)
     for f in range(SWEEPS):
+        ready(f, 0)
+        ready(f, 1)
         top = None
-        for x, field in take(f):
-            field = jnp.max(jnp.abs(field).reshape(32, 8, CELLS), axis=0)
-            top = field if top is None else jnp.maximum(top, field)
+        for x in range(4):
+            part = jnp.concatenate([plane(f, h, x) for h in range(2)], 1)
+            part = matmul(left[...], split(part, 0))
+            part = matmul(split_halves(part[:, :128], part[:, 128:]), right[...])
+            part = jnp.max(jnp.abs(part).reshape(32, 8, CELLS), axis=0)
+            top = part if top is None else jnp.maximum(top, part)
         peaks = jnp.where(lane == f, jnp.max(top), peaks)
     peak_sent[...] = peaks
 
-    others(
+    far_first(
         lambda t: pltpu.make_async_remote_copy(
             peak_sent, peak_got.at[me], psend_sem, pgot_sem, device_id=t, device_id_type=MESH
         ).start()
     )
     peak_got[me] = peaks
-    give(SWEEPS, 1, 2, 4)
-    for x, field in take(SWEEPS):
-        out[x] = field
-        pltpu.make_async_copy(out.at[x], out_hbm.at[0, x], out_sem.at[x]).start()
-
+    give(SWEEPS, 1, far_first, 48, DEVS - 1)
+    ready(SWEEPS, 0)
+    for x, part in pairs(0):
+        base[x] = matmul(split(part, 1), right[pl.ds(0, 384), :])
     all_but_one(peak_got, DEVS, pgot_sem)
-    peaks = jnp.max(peak_got[...], axis=0)
-    for f in range(SWEEPS):
-        res_ref[f] = jnp.max(jnp.where(lane == f, peaks, 0.0))
-
+    peak[...] = jnp.max(peak_got[...], axis=0)
     for h in range(2):
         all_but_one(sent0.at[h], SLABS, send0_sem.at[h])
         all_but_one(sent.at[h], DEVS, send_sem.at[h])
         for f in range(FIELDS):
             all_but_one(bsent.at[f, h], DEVS, bsend_sem.at[f, h])
     all_but_one(peak_got, DEVS, psend_sem)
+    loads[9].wait()
+    ready(SWEEPS, 1)
+    for x, part in pairs(1):
+        last[x] = part
+
+
+def finish(base, last, peak, right_b, out_hbm, res_hbm, out, res, out_sem):
+    copies = [pltpu.make_async_copy(out.at[x], out_hbm.at[0, x], out_sem.at[x]) for x in range(4)]
     for x in range(4):
-        pltpu.make_async_copy(out.at[x], out_hbm.at[0, x], out_sem.at[x]).wait()
+        out[x] = base[x] + matmul(split(last[x], 1), right_b[...])
+        copies[x].start()
+        if x == 0:
+            lane = lax.broadcasted_iota(jnp.int32, (1, 128), 1)
+            for f in range(SWEEPS):
+                res[f] = jnp.max(jnp.where(lane == f, peak[...], 0.0))
+            copies.append(pltpu.make_async_copy(res, res_hbm, out_sem.at[4]))
+            copies[4].start()
+    for copy in copies:
+        copy.wait()
 
 
 def on_device(initial, sections):
     points, quadrature = radau_tables(NODES)
     any_space = pl.BlockSpec(memory_space=pl.ANY)
-    smem = pl.BlockSpec(memory_space=pltpu.SMEM)
     dma = pltpu.SemaphoreType.DMA
     parts = [jnp.asarray(t) for t in tables()]
     vmem = pltpu.VMEM
-    new, peak = pl.pallas_call(
+    whole = pl.BlockSpec(memory_space=pltpu.VMEM)
+    pinned = pl.BlockSpec(memory_space=pltpu.HBM)
+    found = pl.pallas_call(
         functools.partial(kernel, points, quadrature),
         out_shape=(
-            jax.ShapeDtypeStruct(sections.shape, F32),
-            jax.ShapeDtypeStruct((SWEEPS,), F32),
+            jax.ShapeDtypeStruct((4, CELLS, CELLS), F32),
+            jax.ShapeDtypeStruct((4, CELLS, 128), F32),
+            jax.ShapeDtypeStruct((1, 128), F32),
+            jax.ShapeDtypeStruct((384, CELLS), BF16),
         ),
-        in_specs=[any_space] * 9,
-        out_specs=(any_space, smem),
+        in_specs=[pinned] * 9,
+        out_specs=(whole,) * 4,
         scratch_shapes=[
             vmem((4, CELLS, CELLS), F32),
             vmem((4, CELLS, CELLS), F32),
@@ -358,13 +399,12 @@
             vmem((2, SLABS, 8, 128), F32),
             vmem((128, NODES * 128), F32),
             vmem((128, 128), F32),
-            vmem((FIELDS, 128, NODES * 128), F32),
+            vmem((128, NODES * 128), F32),
             vmem((FIELDS, 2, DEVS, 8, 128), F32),
             vmem((FIELDS, 2, DEVS, 8, 128), F32),
-            vmem((4, CELLS, CELLS), F32),
             vmem((1, 128), F32),
             vmem((DEVS, 1, 128), F32),
-            dma((9,)),
+            dma((10,)),
             dma((2,)),
             dma((2,)),
             dma((2,)),
@@ -373,14 +413,24 @@
             dma((FIELDS, 2)),
             dma,
             dma,
-            dma((4,)),
         ],
         compiler_params=pltpu.CompilerParams(
-            collective_id=0, has_side_effects=True, vmem_limit_bytes=67043328
+            collective_id=0, has_side_effects=True, vmem_limit_bytes=30 << 20
         ),
         name="sdc",
-    )(sections, initial, *parts)
-    return new, peak
+    )(*(pltpu.with_memory_space_constraint(value, pltpu.HBM) for value in (sections, initial, *parts)))
+    return pl.pallas_call(
+        finish,
+        out_shape=(
+            jax.ShapeDtypeStruct(sections.shape, F32),
+            jax.ShapeDtypeStruct((SWEEPS,), F32),
+        ),
+        in_specs=[whole] * 4,
+        out_specs=(any_space, any_space),
+        scratch_shapes=[vmem((4, CELLS, CELLS), F32), pltpu.SMEM((SWEEPS,), F32), dma((5,))],
+        compiler_params=pltpu.CompilerParams(vmem_limit_bytes=16 << 20),
+        name="finish",
+    )(*found)
 
 
 def solution(mesh):

time: 79.8 us -> 75.1 us (0.941)
  local copies, waits for them, and re-layouts: 2.8 us -> 0 us
  Pallas kernels: 76.2 us -> 74.2 us
    pallas_call x1, Pallas kernels: 76.2 us -> 72.9 us  [on_device(): pl.pallas_call(functools.partial(kernel, points, quadrature), out_shape=(...]
    unnamed x4 -> x0, local copies, waits for them, and re-layouts: 2.8 us -> none
    pallas_call x0 -> x1, Pallas kernels: none -> 1.33 us  [on_device(): pl.pallas_call(finish, out_shape=(jax.ShapeDtypeStruct(sections.shape, F3...]
where the time goes in v2:
time: 75.1 us; the launch traced here: 75 us
  Pallas kernels  74.2 us (99%)
  between operations  0.8 us (1%)
    pallas_call x1, Pallas kernels, on_device(): pl.pallas_call(functools.partial(kernel, points, quadrature), out_shape=(...  72.9 us

profile of v2, /device:TPU:1, one launch (start us, length us, event | category | flops | bytes accessed | tf_op | source)
XLA Modules:
  0.0 75.0 jit_solution(12892088032819805590)
XLA Ops:
  0.6 72.9 %sdc.1 = (f32[4,256,256]{2,1,0:T(8,128)S(1)}, f32[4,256,128]{2,1,0:T(8,128)S(1)}, f32[1,128]{1,0:T(1,128)S(1)}, bf16[384,256]{1,0:T(8,128)(2,1)S(1)}) custom-call(f32[1,4,256,256]{3,2,1,0:T(8,128)} %sec_hbm.1, f32[4,256,256]{2,1,0:T(8,128)} %ini_hbm.1, bf16[768,256]{1,0:T(8,128)(2,1)} %constant.14.clone.right_hbm, bf16[256,768]{1,0:T(8,128)(2,1)} %constant.15.clone.left_hbm, ...), custom_call_target="tpu_custom_call" | custom-call | tf_op jit(solution)/shard_map/sdc/pallas_call | solution.py:374
  73.5 1.3 %finish.1 = (f32[1,4,256,256]{3,2,1,0:T(8,128)}, f32[3]{0:T(128)}) custom-call(f32[4,256,256]{2,1,0:T(8,128)S(1)} %get-tuple-element.6.base, f32[4,256,128]{2,1,0:T(8,128)S(1)} %get-tuple-element.7.last, f32[1,128]{1,0:T(1,128)S(1)} %get-tuple-element.8.peak, bf16[384,256]{1,0:T(8,128)(2,1)S(1)} %get-tuple-element.9.right_b), custom_call_target="tpu_custom_call" | custom-call | tf_op jit(solution)/shard_map/finish/pallas_call | solution.py:422

commit v3 on v2

--- a/solution.py
+++ b/solution.py
@@ -131,7 +131,7 @@
 def kernel(
     points, quadrature,
     sec_hbm, ini_hbm, right_hbm, left_hbm, fwd_hbm, back_hbm, lam_x_hbm, lam_z_hbm, lam_y_hbm,
-    base, last, peak, right_b,
+    first, last, peak,
     sec, ini, right, left, fwd, back, lam_x, lam_z, lam_y,
     rows, rows0, sent, sent0, got, got0, modes, modes0, spect, bsent, bgot, peak_sent, peak_got,
     in_sem, send_sem, send0_sem, got_sem, got0_sem, bsend_sem, bgot_sem, psend_sem, pgot_sem,
@@ -147,11 +147,8 @@
         for i, (src, dst) in enumerate([
             (left_hbm, left), (sec_hbm.at[0], sec), (right_hbm, right), (ini_hbm, ini), (fwd_hbm, fwd),
             (back_hbm, back), (lam_x_hbm, lam_x), (lam_z_hbm, lam_z), (lam_y_hbm.at[me], lam_y),
-            (right_hbm.at[pl.ds(384, 384)], right_b),
         ])
     ]
-    for load in loads:
-        load.start()
 
     def flat(t):
         return (((t[0] * 4 + t[1]) * 2 + t[2]) * 4 + t[3]) * 2 + t[4]
@@ -162,21 +159,6 @@
     across = [lax.rem(here[3] + k, 4) for k in range(4)]
     depths = [lax.rem(here[1] + k, 4) for k in range(4)]
 
-    def others(visit, low=0, high=4):
-        def step(i, first):
-            along = [lax.rem(here[3] + i + k, 4) for k in range(4)]
-            for k in range(first, 32):
-                y_high, y_low = planes[5 * k % 16 // 4]
-                visit((y_high, depths[5 * k % 4], y_low, along[k % 4], cores[k // 16]))
-
-        def body(i, carry):
-            step(i, 0)
-            return carry
-
-        if low == 0:
-            step(0, 1)
-        lax.fori_loop(max(low, 1), high, body, 0)
-
     def far_first(visit, low=0, high=DEVS - 1):
         for y, z, x, core in FAR_FIRST[low:high]:
             visit((planes[y][0], depths[z], planes[y][1], across[x], cores[core]))
@@ -184,6 +166,9 @@
     barrier = pltpu.get_barrier_semaphore()
 
     far_first(lambda t: pl.semaphore_signal(barrier, inc=1, device_id=t, device_id_type=MESH))
+
+    for load in loads:
+        load.start()
 
     def put(buf, x, count, value):
         for h in range(2):
@@ -201,14 +186,14 @@
             sent[h, pl.ds(32 * b, 32)] = part[:, 128 * h : 128 * h + 128].reshape(32, 8, 128)
     pl.semaphore_wait(barrier, DEVS - 1)
 
-    def spread(src, dst, s_sem, r_sem, order=others, low=None, high=None):
-        order(
+    def spread(src, dst, s_sem, r_sem, low=0, high=DEVS - 1):
+        far_first(
             lambda t: pltpu.make_async_remote_copy(
                 src.at[flat(t)], dst.at[me], s_sem, r_sem, device_id=t, device_id_type=MESH
             ).start(),
-            *(() if low is None else (low, high)),
+            low, high,
         )
-        if not low:
+        if low == 0:
             dst[me] = src[me]
 
     def all_but_one(buf, count, sem):
@@ -235,7 +220,7 @@
         got0[h, my_slab] = sent0[h, my_slab]
     spread(sent.at[1], got.at[1], send_sem.at[1], got_sem.at[1])
 
-    for load in loads[4:9]:
+    for load in loads[4:]:
         load.wait()
 
     def enter(h):
@@ -274,8 +259,18 @@
         for n in range(0, NODES, 2):
             pair = matmul(back[...], split(source[:, 128 * n : 128 * n + 256], 0))
             for k in range(2):
-                block = pair[:, 128 * k : 128 * k + 128].reshape(SLABS, 8, 128)
-                bsent[f, h, pl.ds(SLABS * (n + k), SLABS)] = block
+                block = pair[:, 128 * k : 128 * k + 128]
+                if f < SWEEPS:
+                    bsent[f, h, pl.ds(SLABS * (n + k), SLABS)] = block.reshape(SLABS, 8, 128)
+                else:
+                    rows[h, pl.ds(128 * (n + k), 128), :] = block
+
+    def make_z():
+        for b in range(4):
+            part = split_halves(*(rows[h, pl.ds(CELLS * b, CELLS), :] for h in range(2)))
+            part = matmul(part, right[...])
+            for h in range(2):
+                bsent[SWEEPS, h, pl.ds(32 * b, 32)] = part[:, 128 * h : 128 * h + 128].reshape(32, 8, 128)
 
     def give(f, h, *how):
         spread(bsent.at[f, h], bgot.at[f, h], bsend_sem.at[f, h], bgot_sem.at[f, h], *how)
@@ -292,9 +287,11 @@
         if f < SWEEPS:
             sweep(f, 1)
         make(f, 1)
+        if f == SWEEPS:
+            make_z()
         if f >= 2:
             give(f, 0)
-        give(f, 1, *(() if f < SWEEPS else (far_first, 0, 48)))
+        give(f, 1, *(() if f < SWEEPS else (0, 72)))
 
     def ready(f, h):
         all_but_one(bgot.at[f, h], DEVS, bgot_sem.at[f, h])
@@ -330,10 +327,10 @@
         ).start()
     )
     peak_got[me] = peaks
-    give(SWEEPS, 1, far_first, 48, DEVS - 1)
+    give(SWEEPS, 1, 72, DEVS - 1)
     ready(SWEEPS, 0)
     for x, part in pairs(0):
-        base[x] = matmul(split(part, 1), right[pl.ds(0, 384), :])
+        first[x] = part
     all_but_one(peak_got, DEVS, pgot_sem)
     peak[...] = jnp.max(peak_got[...], axis=0)
     for h in range(2):
@@ -342,23 +339,23 @@
         for f in range(FIELDS):
             all_but_one(bsent.at[f, h], DEVS, bsend_sem.at[f, h])
     all_but_one(peak_got, DEVS, psend_sem)
-    loads[9].wait()
     ready(SWEEPS, 1)
     for x, part in pairs(1):
         last[x] = part
 
 
-def finish(base, last, peak, right_b, out_hbm, res_hbm, out, res, out_sem):
-    copies = [pltpu.make_async_copy(out.at[x], out_hbm.at[0, x], out_sem.at[x]) for x in range(4)]
-    for x in range(4):
-        out[x] = base[x] + matmul(split(last[x], 1), right_b[...])
-        copies[x].start()
-        if x == 0:
-            lane = lax.broadcasted_iota(jnp.int32, (1, 128), 1)
-            for f in range(SWEEPS):
-                res[f] = jnp.max(jnp.where(lane == f, peak[...], 0.0))
-            copies.append(pltpu.make_async_copy(res, res_hbm, out_sem.at[4]))
-            copies[4].start()
+def finish(first, last, peak, out_hbm, res_hbm, res, out_sem):
+    copies = [
+        pltpu.make_async_copy(part, out_hbm.at[0, :, :, pl.ds(128 * h, 128)], out_sem.at[h])
+        for h, part in enumerate((first, last))
+    ]
+    for copy in copies:
+        copy.start()
+    lane = lax.broadcasted_iota(jnp.int32, (1, 128), 1)
+    for f in range(SWEEPS):
+        res[f] = jnp.max(jnp.where(lane == f, peak[...], 0.0))
+    copies.append(pltpu.make_async_copy(res, res_hbm, out_sem.at[2]))
+    copies[2].start()
     for copy in copies:
         copy.wait()
 
@@ -374,13 +371,12 @@
     found = pl.pallas_call(
         functools.partial(kernel, points, quadrature),
         out_shape=(
-            jax.ShapeDtypeStruct((4, CELLS, CELLS), F32),
+            jax.ShapeDtypeStruct((4, CELLS, 128), F32),
             jax.ShapeDtypeStruct((4, CELLS, 128), F32),
             jax.ShapeDtypeStruct((1, 128), F32),
-            jax.ShapeDtypeStruct((384, CELLS), BF16),
         ),
         in_specs=[pinned] * 9,
-        out_specs=(whole,) * 4,
+        out_specs=(whole,) * 3,
         scratch_shapes=[
             vmem((4, CELLS, CELLS), F32),
             vmem((4, CELLS, CELLS), F32),
@@ -404,7 +400,7 @@
             vmem((FIELDS, 2, DEVS, 8, 128), F32),
             vmem((1, 128), F32),
             vmem((DEVS, 1, 128), F32),
-            dma((10,)),
+            dma((9,)),
             dma((2,)),
             dma((2,)),
             dma((2,)),
@@ -425,9 +421,9 @@
             jax.ShapeDtypeStruct(sections.shape, F32),
             jax.ShapeDtypeStruct((SWEEPS,), F32),
         ),
-        in_specs=[whole] * 4,
+        in_specs=[whole] * 3,
         out_specs=(any_space, any_space),
-        scratch_shapes=[vmem((4, CELLS, CELLS), F32), pltpu.SMEM((SWEEPS,), F32), dma((5,))],
+        scratch_shapes=[pltpu.SMEM((SWEEPS,), F32), dma((3,))],
         compiler_params=pltpu.CompilerParams(vmem_limit_bytes=16 << 20),
         name="finish",
     )(*found)

time: 75.1 us -> 74.2 us (0.988)
  Pallas kernels: 74.2 us -> 73.3 us
where the time goes in v3:
time: 74.2 us; the launch traced here: 74.1 us
  Pallas kernels  73.3 us (99%)
  between operations  0.8 us (1%)
    pallas_call x1, Pallas kernels, on_device(): pl.pallas_call(functools.partial(kernel, points, quadrature), out_shape=(...  72.3 us

profile of v3, /device:TPU:1, one launch (start us, length us, event | category | flops | bytes accessed | tf_op | source)
XLA Modules:
  0.0 74.1 jit_solution(1598141627338516009)
XLA Ops:
  0.6 72.3 %sdc.1 = (f32[4,256,128]{2,1,0:T(8,128)S(1)}, f32[4,256,128]{2,1,0:T(8,128)S(1)}, f32[1,128]{1,0:T(1,128)S(1)}) custom-call(f32[1,4,256,256]{3,2,1,0:T(8,128)} %sec_hbm.1, f32[4,256,256]{2,1,0:T(8,128)} %ini_hbm.1, bf16[768,256]{1,0:T(8,128)(2,1)} %constant.14.clone.right_hbm, bf16[256,768]{1,0:T(8,128)(2,1)} %constant.15.clone.left_hbm, ...), custom_call_target="tpu_custom_call" | custom-call | tf_op jit(solution)/shard_map/sdc/pallas_call | solution.py:371
  72.9 1.0 %finish.1 = (f32[1,4,256,256]{3,2,1,0:T(8,128)}, f32[3]{0:T(128)}) custom-call(f32[4,256,128]{2,1,0:T(8,128)S(1)} %get-tuple-element.5.first, f32[4,256,128]{2,1,0:T(8,128)S(1)} %get-tuple-element.6.last, f32[1,128]{1,0:T(1,128)S(1)} %get-tuple-element.7.peak), custom_call_target="tpu_custom_call" | custom-call | tf_op jit(solution)/shard_map/finish/pallas_call | solution.py:418

commit v4 on v3

--- a/solution.py
+++ b/solution.py
@@ -133,7 +133,7 @@
     sec_hbm, ini_hbm, right_hbm, left_hbm, fwd_hbm, back_hbm, lam_x_hbm, lam_z_hbm, lam_y_hbm,
     first, last, peak,
     sec, ini, right, left, fwd, back, lam_x, lam_z, lam_y,
-    rows, rows0, sent, sent0, got, got0, modes, modes0, spect, bsent, bgot, peak_sent, peak_got,
+    rows, rows0, sent, sent0, got, got0, modes, modes0, spect, bsent, bgot, peak_sent, peak_got, peak_all,
     in_sem, send_sem, send0_sem, got_sem, got0_sem, bsend_sem, bgot_sem, psend_sem, pgot_sem,
 ):
     here = tuple(lax.axis_index(a) for a in AXES)
@@ -159,8 +159,8 @@
     across = [lax.rem(here[3] + k, 4) for k in range(4)]
     depths = [lax.rem(here[1] + k, 4) for k in range(4)]
 
-    def far_first(visit, low=0, high=DEVS - 1):
-        for y, z, x, core in FAR_FIRST[low:high]:
+    def far_first(visit):
+        for y, z, x, core in FAR_FIRST:
             visit((planes[y][0], depths[z], planes[y][1], across[x], cores[core]))
 
     barrier = pltpu.get_barrier_semaphore()
@@ -177,24 +177,22 @@
     loads[0].wait()
     loads[1].wait()
     for x in range(4):
-        put(rows, x, CELLS, matmul(left[...], split(sec[x], 0)))
+        put(rows.at[0], x, CELLS, matmul(left[...], split(sec[x], 0)))
     loads[2].wait()
     for b in range(4):
-        part = split_halves(*(rows[h, pl.ds(CELLS * b, CELLS), :] for h in range(2)))
+        part = split_halves(*(rows[0, h, pl.ds(CELLS * b, CELLS), :] for h in range(2)))
         part = matmul(part, right[...])
         for h in range(2):
             sent[h, pl.ds(32 * b, 32)] = part[:, 128 * h : 128 * h + 128].reshape(32, 8, 128)
     pl.semaphore_wait(barrier, DEVS - 1)
 
-    def spread(src, dst, s_sem, r_sem, low=0, high=DEVS - 1):
+    def spread(src, dst, s_sem, r_sem):
         far_first(
             lambda t: pltpu.make_async_remote_copy(
                 src.at[flat(t)], dst.at[me], s_sem, r_sem, device_id=t, device_id_type=MESH
-            ).start(),
-            low, high,
+            ).start()
         )
-        if low == 0:
-            dst[me] = src[me]
+        dst[me] = src[me]
 
     def all_but_one(buf, count, sem):
         view = buf.at[pl.ds(0, count - 1)]
@@ -260,20 +258,20 @@
             pair = matmul(back[...], split(source[:, 128 * n : 128 * n + 256], 0))
             for k in range(2):
                 block = pair[:, 128 * k : 128 * k + 128]
-                if f < SWEEPS:
+                if f < 2:
                     bsent[f, h, pl.ds(SLABS * (n + k), SLABS)] = block.reshape(SLABS, 8, 128)
                 else:
-                    rows[h, pl.ds(128 * (n + k), 128), :] = block
-
-    def make_z():
+                    rows[f - 2, h, pl.ds(128 * (n + k), 128), :] = block
+
+    def make_z(f):
         for b in range(4):
-            part = split_halves(*(rows[h, pl.ds(CELLS * b, CELLS), :] for h in range(2)))
+            part = split_halves(*(rows[f - 2, h, pl.ds(CELLS * b, CELLS), :] for h in range(2)))
             part = matmul(part, right[...])
             for h in range(2):
-                bsent[SWEEPS, h, pl.ds(32 * b, 32)] = part[:, 128 * h : 128 * h + 128].reshape(32, 8, 128)
-
-    def give(f, h, *how):
-        spread(bsent.at[f, h], bgot.at[f, h], bsend_sem.at[f, h], bgot_sem.at[f, h], *how)
+                bsent[f, h, pl.ds(32 * b, 32)] = part[:, 128 * h : 128 * h + 128].reshape(32, 8, 128)
+
+    def give(f, h):
+        spread(bsent.at[f, h], bgot.at[f, h], bsend_sem.at[f, h], bgot_sem.at[f, h])
 
     enter(0)
     for f in range(FIELDS):
@@ -287,11 +285,11 @@
         if f < SWEEPS:
             sweep(f, 1)
         make(f, 1)
-        if f == SWEEPS:
-            make_z()
         if f >= 2:
+            make_z(f)
             give(f, 0)
-        give(f, 1, *(() if f < SWEEPS else (0, 72)))
+        if f < SWEEPS:
+            give(f, 1)
 
     def ready(f, h):
         all_but_one(bgot.at[f, h], DEVS, bgot_sem.at[f, h])
@@ -299,48 +297,67 @@
     def plane(f, h, x):
         return bgot.at[f, h].reshape(4 * CELLS, 128)[pl.ds(x, CELLS, stride=4), :]
 
-    def pairs(h):
+    def pairs(f, h):
         for x in range(0, 4, 2):
-            part = jnp.concatenate([plane(SWEEPS, h, x + k) for k in range(2)], 1)
+            part = jnp.concatenate([plane(f, h, x + k) for k in range(2)], 1)
             part = matmul(left[...], split(part, 0))
             yield x, part[:, :128]
             yield x + 1, part[:, 128:]
 
+    def peak_of(parts):
+        parts = [jnp.max(jnp.abs(part).reshape(32, 8, part.shape[1]), axis=0) for part in parts]
+        return jnp.max(functools.reduce(jnp.maximum, parts))
+
     lane = lax.broadcasted_iota(jnp.int32, (1, 128), 1)
     peaks = jnp.zeros((1, 128), F32)
-    for f in range(SWEEPS):
+    for f in range(2):
         ready(f, 0)
         ready(f, 1)
-        top = None
+        parts = []
         for x in range(4):
             part = jnp.concatenate([plane(f, h, x) for h in range(2)], 1)
             part = matmul(left[...], split(part, 0))
-            part = matmul(split_halves(part[:, :128], part[:, 128:]), right[...])
-            part = jnp.max(jnp.abs(part).reshape(32, 8, CELLS), axis=0)
-            top = part if top is None else jnp.maximum(top, part)
-        peaks = jnp.where(lane == f, jnp.max(top), peaks)
-    peak_sent[...] = peaks
-
-    far_first(
-        lambda t: pltpu.make_async_remote_copy(
-            peak_sent, peak_got.at[me], psend_sem, pgot_sem, device_id=t, device_id_type=MESH
+            parts.append(matmul(split_halves(part[:, :128], part[:, 128:]), right[...]))
+        peaks = jnp.where(lane == f, peak_of(parts), peaks)
+    for h in range(2):
+        ready(2, h)
+        top = peak_of([part for x, part in pairs(2, h)])
+        peaks = jnp.maximum(peaks, jnp.where(lane == 2, top, 0.0))
+    peak_sent[0] = peaks
+
+    place = here[1] * 4 + here[3]
+    for k in range(1, 16):
+        pltpu.make_async_remote_copy(
+            peak_sent.at[0], peak_got.at[place], psend_sem.at[0], pgot_sem.at[0],
+            device_id=(here[0], depths[k // 4], here[2], across[k % 4], here[4]), device_id_type=MESH,
         ).start()
-    )
-    peak_got[me] = peaks
-    give(SWEEPS, 1, 72, DEVS - 1)
+    peak_got[place] = peaks
+    give(SWEEPS, 1)
     ready(SWEEPS, 0)
-    for x, part in pairs(0):
+    for x, part in pairs(SWEEPS, 0):
         first[x] = part
-    all_but_one(peak_got, DEVS, pgot_sem)
-    peak[...] = jnp.max(peak_got[...], axis=0)
+    all_but_one(peak_got, 16, pgot_sem.at[0])
+    peaks = jnp.max(peak_got[...], axis=0)
+    peak_sent[1] = peaks
+    place = my_y * 2 + here[4]
+    for k in range(1, 8):
+        pltpu.make_async_remote_copy(
+            peak_sent.at[1], peak_all.at[place], psend_sem.at[1], pgot_sem.at[1],
+            device_id=(planes[k // 2][0], here[1], planes[k // 2][1], here[3], cores[k % 2]),
+            device_id_type=MESH,
+        ).start()
+    peak_all[place] = peaks
+    all_but_one(peak_all, 8, pgot_sem.at[1])
+    peak[...] = jnp.max(peak_all[...], axis=0)
     for h in range(2):
         all_but_one(sent0.at[h], SLABS, send0_sem.at[h])
         all_but_one(sent.at[h], DEVS, send_sem.at[h])
         for f in range(FIELDS):
             all_but_one(bsent.at[f, h], DEVS, bsend_sem.at[f, h])
-    all_but_one(peak_got, DEVS, psend_sem)
+    all_but_one(peak_got, 16, psend_sem.at[0])
+    all_but_one(peak_all, 8, psend_sem.at[1])
     ready(SWEEPS, 1)
-    for x, part in pairs(1):
+    for x, part in pairs(SWEEPS, 1):
         last[x] = part
 
 
@@ -387,7 +404,7 @@
             vmem((64, 128), F32),
             vmem((2, 8, 128), F32),
             vmem((2, 128), F32),
-            vmem((2, 4 * CELLS, 128), F32),
+            vmem((2, 2, 4 * CELLS, 128), F32),
             vmem((2, 128, 128), F32),
             vmem((2, DEVS, 8, 128), F32),
             vmem((2, SLABS, 8, 128), F32),
@@ -398,8 +415,9 @@
             vmem((128, NODES * 128), F32),
             vmem((FIELDS, 2, DEVS, 8, 128), F32),
             vmem((FIELDS, 2, DEVS, 8, 128), F32),
-            vmem((1, 128), F32),
-            vmem((DEVS, 1, 128), F32),
+            vmem((2, 1, 128), F32),
+            vmem((16, 1, 128), F32),
+            vmem((8, 1, 128), F32),
             dma((9,)),
             dma((2,)),
             dma((2,)),
@@ -407,8 +425,8 @@
             dma((2,)),
             dma((FIELDS, 2)),
             dma((FIELDS, 2)),
-            dma,
-            dma,
+            dma((2,)),
+            dma((2,)),
         ],
         compiler_params=pltpu.CompilerParams(
             collective_id=0, has_side_effects=True, vmem_limit_bytes=30 << 20

time: 74.2 us -> 73.3 us (0.988)
  Pallas kernels: 73.3 us -> 72.3 us
    pallas_call x1, Pallas kernels: 72.3 us -> 71.3 us  [on_device(): pl.pallas_call(functools.partial(kernel, points, quadrature), out_shape=(...]
where the time goes in v4:
time: 73.3 us; the launch traced here: 73.1 us
  Pallas kernels  72.3 us (99%)
  between operations  0.8 us (1%)
    pallas_call x1, Pallas kernels, on_device(): pl.pallas_call(functools.partial(kernel, points, quadrature), out_shape=(...  71.3 us

profile of v4, /device:TPU:1, one launch (start us, length us, event | category | flops | bytes accessed | tf_op | source)
XLA Modules:
  0.0 73.1 jit_solution(3193042315218858499)
XLA Ops:
  0.6 71.3 %sdc.1 = (f32[4,256,128]{2,1,0:T(8,128)S(1)}, f32[4,256,128]{2,1,0:T(8,128)S(1)}, f32[1,128]{1,0:T(1,128)S(1)}) custom-call(f32[1,4,256,256]{3,2,1,0:T(8,128)} %sec_hbm.1, f32[4,256,256]{2,1,0:T(8,128)} %ini_hbm.1, bf16[768,256]{1,0:T(8,128)(2,1)} %constant.14.clone.right_hbm, bf16[256,768]{1,0:T(8,128)(2,1)} %constant.15.clone.left_hbm, ...), custom_call_target="tpu_custom_call" | custom-call | tf_op jit(solution)/shard_map/sdc/pallas_call | solution.py:388
  72.0 1.0 %finish.1 = (f32[1,4,256,256]{3,2,1,0:T(8,128)}, f32[3]{0:T(128)}) custom-call(f32[4,256,128]{2,1,0:T(8,128)S(1)} %get-tuple-element.5.first, f32[4,256,128]{2,1,0:T(8,128)S(1)} %get-tuple-element.6.last, f32[1,128]{1,0:T(1,128)S(1)} %get-tuple-element.7.peak), custom_call_target="tpu_custom_call" | custom-call | tf_op jit(solution)/shard_map/finish/pallas_call | solution.py:436

commit v5 on v4

--- a/solution.py
+++ b/solution.py
@@ -88,26 +88,26 @@
     return -4.0 * np.sin(np.arange(length) * (math.pi / length)) ** 2
 
 
-def halves(table):
-    high = table.astype(np.float32).astype(BF16)
-    low = (table - high.astype(np.float64)).astype(np.float32).astype(BF16)
-    return high, low
+def pieces(table):
+    found = []
+    for k in range(3):
+        found.append(table.astype(np.float32).astype(BF16))
+        table = table - found[-1].astype(np.float64)
+    return found
 
 
 def tables():
     line = cas_table(CELLS)
-    high, low = halves(line)
-    right = np.concatenate([part for h in (slice(0, 128), slice(128, 256)) for part in (high[h], high[h], low[h])], 0)
-    left = np.concatenate([high, high, low], 1)
+    parts = pieces(line)
+    right = np.concatenate([part[h] for h in (slice(0, 128), slice(128, 256)) for part in parts], 0)
+    left = np.concatenate(parts, 1)
     cas_x = cas_table(64)
     cross = np.zeros((2, 64, SLABS, 2, 4))
     for row in range(2):
         cross[row, :, :, row, :] = cas_x.reshape(64, SLABS, 4)
     cross = cross.reshape(128, 128)
-    high, low = halves(cross)
-    forward = np.concatenate([high, high, low], 1)
-    high, low = halves(cross.T)
-    back = np.concatenate([high, high, low], 1)
+    forward = np.concatenate(pieces(cross), 1)
+    back = np.concatenate(pieces(cross.T), 1)
     lam_x = np.broadcast_to((STEP * eigen_line(64))[:, None], (64, 128)).astype(np.float32)
     lam_z = np.broadcast_to((STEP * eigen_line(CELLS)).reshape(2, 1, 128), (2, 8, 128)).astype(np.float32)
     lam_y = np.broadcast_to((STEP * eigen_line(CELLS)).reshape(DEVS, 2, 1), (DEVS, 2, 128)).astype(np.float32)
@@ -118,6 +118,26 @@
     high = value.astype(BF16)
     low = (value - high.astype(F32)).astype(BF16)
     return jnp.concatenate([high, low, high], axis)
+
+
+def split_fine(value, axis):
+    high = value.astype(BF16)
+    value = value - high.astype(F32)
+    mid = value.astype(BF16)
+    low = (value - mid.astype(F32)).astype(BF16)
+    return jnp.concatenate([high, high, mid, high, mid, low], axis)
+
+
+ROUGH = (0, 0, 1)
+FINE = (0, 1, 0, 2, 1, 0)
+
+
+def across(ref, order, width, rows=slice(None)):
+    return jnp.concatenate([ref[rows, width * k : width * k + width] for k in order], 1)
+
+
+def down(ref, order):
+    return jnp.concatenate([ref[384 * h + 128 * k : 384 * h + 128 * k + 128, :] for h in range(2) for k in order], 0)
 
 
 def split_halves(first, second):
@@ -156,19 +176,18 @@
     cores = (here[4], 1 - here[4])
     planes = [lax.rem(my_y + k, 4) for k in range(4)]
     planes = [(y // 2, lax.rem(y, 2)) for y in planes]
-    across = [lax.rem(here[3] + k, 4) for k in range(4)]
+    widths = [lax.rem(here[3] + k, 4) for k in range(4)]
     depths = [lax.rem(here[1] + k, 4) for k in range(4)]
 
     def far_first(visit):
         for y, z, x, core in FAR_FIRST:
-            visit((planes[y][0], depths[z], planes[y][1], across[x], cores[core]))
+            visit((planes[y][0], depths[z], planes[y][1], widths[x], cores[core]))
 
     barrier = pltpu.get_barrier_semaphore()
-
-    far_first(lambda t: pl.semaphore_signal(barrier, inc=1, device_id=t, device_id_type=MESH))
 
     for load in loads:
         load.start()
+    far_first(lambda t: pl.semaphore_signal(barrier, inc=1, device_id=t, device_id_type=MESH))
 
     def put(buf, x, count, value):
         for h in range(2):
@@ -177,11 +196,11 @@
     loads[0].wait()
     loads[1].wait()
     for x in range(4):
-        put(rows.at[0], x, CELLS, matmul(left[...], split(sec[x], 0)))
+        put(rows.at[0], x, CELLS, matmul(across(left, FINE, CELLS), split_fine(sec[x], 0)))
     loads[2].wait()
     for b in range(4):
-        part = split_halves(*(rows[0, h, pl.ds(CELLS * b, CELLS), :] for h in range(2)))
-        part = matmul(part, right[...])
+        part = [split_fine(rows[0, h, pl.ds(CELLS * b, CELLS), :], 1) for h in range(2)]
+        part = matmul(jnp.concatenate(part, 1), down(right, FINE))
         for h in range(2):
             sent[h, pl.ds(32 * b, 32)] = part[:, 128 * h : 128 * h + 128].reshape(32, 8, 128)
     pl.semaphore_wait(barrier, DEVS - 1)
@@ -200,10 +219,11 @@
 
     spread(sent.at[0], got.at[0], send_sem.at[0], got_sem.at[0])
     loads[3].wait()
-    mine = left[pl.ds(pl.multiple_of(my_node * 32, 32), 32), :]
+    mine = across(left, FINE, CELLS, pl.ds(pl.multiple_of(my_node * 32, 32), 32))
     for x in range(4):
-        put(rows0, x, 32, matmul(mine, split(ini[x], 0)))
-    part = matmul(split_halves(rows0[0], rows0[1]), right[...])
+        put(rows0, x, 32, matmul(mine, split_fine(ini[x], 0)))
+    part = jnp.concatenate([split_fine(rows0[h], 1) for h in range(2)], 1)
+    part = matmul(part, down(right, FINE))
     for h in range(2):
         sent0[h] = part[:, 128 * h : 128 * h + 128].reshape(16, 8, 128)
 
@@ -224,10 +244,10 @@
     def enter(h):
         all_but_one(got0.at[h], SLABS, got0_sem.at[h])
         all_but_one(got.at[h], DEVS, got_sem.at[h])
-        modes0[...] = matmul(fwd[...], split(got0[h].reshape(128, 128), 0))
+        modes0[...] = matmul(across(fwd, FINE, 128), split_fine(got0[h].reshape(128, 128), 0))
         for n in range(0, NODES, 2):
             pair = [got[h, pl.ds(SLABS * (n + k), SLABS)].reshape(128, 128) for k in range(2)]
-            modes[:, 128 * n : 128 * n + 256] = matmul(fwd[...], split(jnp.concatenate(pair, 1), 0))
+            modes[:, 128 * n : 128 * n + 256] = matmul(across(fwd, FINE, 128), split_fine(jnp.concatenate(pair, 1), 0))
 
     def sweep(k, h):
         lam_0 = [lam_z[h] + lam_y[row : row + 1, :] for row in range(2)]
@@ -255,7 +275,7 @@
     def make(f, h):
         source = spect if f < SWEEPS else modes
         for n in range(0, NODES, 2):
-            pair = matmul(back[...], split(source[:, 128 * n : 128 * n + 256], 0))
+            pair = matmul(across(back, ROUGH, 128), split(source[:, 128 * n : 128 * n + 256], 0))
             for k in range(2):
                 block = pair[:, 128 * k : 128 * k + 128]
                 if f < 2:
@@ -266,7 +286,7 @@
     def make_z(f):
         for b in range(4):
             part = split_halves(*(rows[f - 2, h, pl.ds(CELLS * b, CELLS), :] for h in range(2)))
-            part = matmul(part, right[...])
+            part = matmul(part, down(right, ROUGH))
             for h in range(2):
                 bsent[f, h, pl.ds(32 * b, 32)] = part[:, 128 * h : 128 * h + 128].reshape(32, 8, 128)
 
@@ -300,7 +320,7 @@
     def pairs(f, h):
         for x in range(0, 4, 2):
             part = jnp.concatenate([plane(f, h, x + k) for k in range(2)], 1)
-            part = matmul(left[...], split(part, 0))
+            part = matmul(across(left, ROUGH, CELLS), split(part, 0))
             yield x, part[:, :128]
             yield x + 1, part[:, 128:]
 
@@ -316,8 +336,8 @@
         parts = []
         for x in range(4):
             part = jnp.concatenate([plane(f, h, x) for h in range(2)], 1)
-            part = matmul(left[...], split(part, 0))
-            parts.append(matmul(split_halves(part[:, :128], part[:, 128:]), right[...]))
+            part = matmul(across(left, ROUGH, CELLS), split(part, 0))
+            parts.append(matmul(split_halves(part[:, :128], part[:, 128:]), down(right, ROUGH)))
         peaks = jnp.where(lane == f, peak_of(parts), peaks)
     for h in range(2):
         ready(2, h)
@@ -329,7 +349,7 @@
     for k in range(1, 16):
         pltpu.make_async_remote_copy(
             peak_sent.at[0], peak_got.at[place], psend_sem.at[0], pgot_sem.at[0],
-            device_id=(here[0], depths[k // 4], here[2], across[k % 4], here[4]), device_id_type=MESH,
+            device_id=(here[0], depths[k // 4], here[2], widths[k % 4], here[4]), device_id_type=MESH,
         ).start()
     peak_got[place] = peaks
     give(SWEEPS, 1)

time: 73.3 us -> 73.2 us (level)
  no operation moved by 1% of the time
where the time goes in v5:
time: 73.2 us; the launch traced here: 73 us
  Pallas kernels  72.2 us (99%)
  between operations  0.8 us (1%)
    pallas_call x1, Pallas kernels, on_device(): pl.pallas_call(functools.partial(kernel, points, quadrature), out_shape=(...  71.2 us

profile of v5, /device:TPU:1, one launch (start us, length us, event | category | flops | bytes accessed | tf_op | source)
XLA Modules:
  0.0 73.0 jit_solution(11232253887703492683)
XLA Ops:
  0.6 71.2 %sdc.1 = (f32[4,256,128]{2,1,0:T(8,128)S(1)}, f32[4,256,128]{2,1,0:T(8,128)S(1)}, f32[1,128]{1,0:T(1,128)S(1)}) custom-call(f32[1,4,256,256]{3,2,1,0:T(8,128)} %sec_hbm.1, f32[4,256,256]{2,1,0:T(8,128)} %ini_hbm.1, bf16[768,256]{1,0:T(8,128)(2,1)} %constant.14.clone.right_hbm, bf16[256,768]{1,0:T(8,128)(2,1)} %constant.15.clone.left_hbm, ...), custom_call_target="tpu_custom_call" | custom-call | tf_op jit(solution)/shard_map/sdc/pallas_call | solution.py:408
  71.9 1.0 %finish.1 = (f32[1,4,256,256]{3,2,1,0:T(8,128)}, f32[3]{0:T(128)}) custom-call(f32[4,256,128]{2,1,0:T(8,128)S(1)} %get-tuple-element.5.first, f32[4,256,128]{2,1,0:T(8,128)S(1)} %get-tuple-element.6.last, f32[1,128]{1,0:T(1,128)S(1)} %get-tuple-element.7.peak), custom_call_target="tpu_custom_call" | custom-call | tf_op jit(solution)/shard_map/finish/pallas_call | solution.py:456

commit v6 on v5

--- a/solution.py
+++ b/solution.py
@@ -353,9 +353,6 @@
         ).start()
     peak_got[place] = peaks
     give(SWEEPS, 1)
-    ready(SWEEPS, 0)
-    for x, part in pairs(SWEEPS, 0):
-        first[x] = part
     all_but_one(peak_got, 16, pgot_sem.at[0])
     peaks = jnp.max(peak_got[...], axis=0)
     peak_sent[1] = peaks
@@ -367,6 +364,9 @@
             device_id_type=MESH,
         ).start()
     peak_all[place] = peaks
+    ready(SWEEPS, 0)
+    for x, part in pairs(SWEEPS, 0):
+        first[x] = part
     all_but_one(peak_all, 8, pgot_sem.at[1])
     peak[...] = jnp.max(peak_all[...], axis=0)
     for h in range(2):

time: 73.2 us -> 73.2 us (level)
  no operation moved by 1% of the time
where the time goes in v6:
time: 73.2 us; the launch traced here: 73 us
  Pallas kernels  72.2 us (99%)
  between operations  0.8 us (1%)
    pallas_call x1, Pallas kernels, on_device(): pl.pallas_call(functools.partial(kernel, points, quadrature), out_shape=(...  71.2 us

profile of v6, /device:TPU:1, one launch (start us, length us, event | category | flops | bytes accessed | tf_op | source)
XLA Modules:
  0.0 73.0 jit_solution(16309287038516856170)
XLA Ops:
  0.6 71.2 %sdc.1 = (f32[4,256,128]{2,1,0:T(8,128)S(1)}, f32[4,256,128]{2,1,0:T(8,128)S(1)}, f32[1,128]{1,0:T(1,128)S(1)}) custom-call(f32[1,4,256,256]{3,2,1,0:T(8,128)} %sec_hbm.1, f32[4,256,256]{2,1,0:T(8,128)} %ini_hbm.1, bf16[768,256]{1,0:T(8,128)(2,1)} %constant.14.clone.right_hbm, bf16[256,768]{1,0:T(8,128)(2,1)} %constant.15.clone.left_hbm, ...), custom_call_target="tpu_custom_call" | custom-call | tf_op jit(solution)/shard_map/sdc/pallas_call | solution.py:408
  71.9 1.0 %finish.1 = (f32[1,4,256,256]{3,2,1,0:T(8,128)}, f32[3]{0:T(128)}) custom-call(f32[4,256,128]{2,1,0:T(8,128)S(1)} %get-tuple-element.5.first, f32[4,256,128]{2,1,0:T(8,128)S(1)} %get-tuple-element.6.last, f32[1,128]{1,0:T(1,128)S(1)} %get-tuple-element.7.peak), custom_call_target="tpu_custom_call" | custom-call | tf_op jit(solution)/shard_map/finish/pallas_call | solution.py:456
